TPU v7x, 128 devices: a whole 4x4x4 slice. The times are simulated.
128 devices in a mesh: blk: 64 (over x, z, y_lo, core), ep: 2 (over y_hi).
Axes of the slice: x: 4, y: 4 (y_hi: 2, y_lo: 2; y = y_hi * 2 + y_lo), z: 4, core: 2. Of those that a mesh axis runs over, the one named last changes fastest.
Arguments:
- hidden_in: bfloat16 [1024, 4096], P('blk'), may hold values from -6 to 6
- out_grad: bfloat16 [1024, 4096], P('blk'), may hold values from -6 to 6
- expert_ids: int32 [1024, 2], P('blk'), may hold values from 0 to 3, all different within a row; in each aligned block of 16 rows (0 to 15, 16 to 31, ...) at most 12 rows name the same one
- gate_values: bfloat16 [1024, 2], P('blk'), may hold values from 0.099609375 to 1
- w_gate: bfloat16 [4, 14336, 4096], P('ep', 'blk'), may hold values from -0.09375 to 0.09375
- w_up: bfloat16 [4, 14336, 4096], P('ep', 'blk'), may hold values from -0.09375 to 0.09375
- w_down: bfloat16 [4, 14336, 4096], P('ep', 'blk'), may hold values from -0.046875 to 0.046875
Outputs:
- input_grad: bfloat16 [1024, 4096], P('blk')
- gate_grad: float32 [1024, 2], P('blk')
- grad_gate: bfloat16 [4, 14336, 4096], P('ep', 'blk')
- grad_up: bfloat16 [4, 14336, 4096], P('ep', 'blk')
- grad_down: bfloat16 [4, 14336, 4096], P('ep', 'blk')
Inputs may be any that keep to these rules, and one draw needn't show every extreme that they name: `expert_ids`: each row names 2 different experts; in each aligned block of 16 rows (the rows of one device) no expert is named by more than 12 rows, a bound that some block reaches.
All inputs are finite; a program needn't handle non-finite values.
Results may differ from a plain program's by a relative error of at most 0.008.
Values may be sent and summed in bfloat16 or wider, within the bound.
No kernel may reach another device: no remote copies, remote signals or barrier semaphores. Data moves between devices by JAX's collectives and lax.ppermute only.
A program may use at most 256 MiB of HBM per device.

v0:
```python
import jax
import jax.numpy as jnp
from jax import lax
from jax.sharding import PartitionSpec as P

TOK_DEV = 16
CAP = 12


def sent_together(arrays, axis, dim, along):
    ends, at = ([], 0)
    for a in arrays[:-1]:
        at += a.shape[along]
        ends.append(at)
    both = jnp.concatenate(arrays, axis=along)
    return tuple(jnp.split(lax.all_gather(both, axis, axis=dim, tiled=True), ends, axis=along))


def side_by_side(arrays, axis, dim, along):
    both = jnp.concatenate(arrays, axis=along)
    filled, at, gathered = (lax.psum_scatter(both, axis, scatter_dimension=dim, tiled=True), 0, [])
    for a in arrays:
        gathered.append(lax.slice_in_dim(filled, at, at + a.shape[along], axis=along))
        at += a.shape[along]
    return tuple(gathered)


def sent_to_all(value, axis):
    copies = jnp.broadcast_to(value, (lax.axis_size(axis), *value.shape))
    return lax.all_to_all(copies, axis, split_axis=0, concat_axis=0, tiled=True)


def taken_together(value, axis):
    return sent_to_all(value, axis).astype(jnp.float32).sum(axis=0)


def routed(expert_ids, gate_values, expert, blocks):
    chosen = expert_ids == expert
    hits = jnp.any(chosen, axis=1).astype(jnp.int32).reshape(blocks, TOK_DEV)
    weight = jnp.sum(
        jnp.where(chosen, gate_values.astype(jnp.float32), jnp.float32(0.0)), axis=1
    ).reshape(blocks, TOK_DEV)
    position = jnp.cumsum(hits, axis=1) - hits
    slot_index = lax.broadcasted_iota(jnp.int32, (blocks, CAP, TOK_DEV), 1)
    picked = (position[:, None, :] == slot_index) & (hits[:, None, :] > 0)
    selector = jnp.where(picked, jnp.float32(1.0), jnp.float32(0.0))
    return (selector, weight, chosen)


def expert_pass(selector, weight, hidden_in, out_grad, gate_mat, up_mat, down_mat, blocks):
    width = hidden_in.shape[1]
    select_low = selector.astype(jnp.bfloat16)
    x_slots = (
        jnp.einsum(
            "bct,btd->bcd",
            select_low,
            hidden_in.reshape(blocks, TOK_DEV, width),
            preferred_element_type=jnp.float32,
        )
        .astype(jnp.bfloat16)
        .reshape(-1, width)
    )
    dy_slots = (
        jnp.einsum(
            "bct,btd->bcd",
            select_low,
            out_grad.reshape(blocks, TOK_DEV, width),
            preferred_element_type=jnp.float32,
        )
        .astype(jnp.bfloat16)
        .reshape(-1, width)
    )
    slot_weight = jnp.einsum("bct,bt->bc", selector, weight).reshape(-1, 1)
    contract_cols = (((1,), (1,)), ((), ()))
    gate_pre = lax.dot_general(x_slots, gate_mat, contract_cols, preferred_element_type=jnp.float32)
    up_pre = lax.dot_general(x_slots, up_mat, contract_cols, preferred_element_type=jnp.float32)
    back = lax.dot_general(dy_slots, down_mat, contract_cols, preferred_element_type=jnp.float32)
    sigmoid_gate = jax.nn.sigmoid(gate_pre)
    activation = gate_pre * sigmoid_gate * up_pre
    slot_gate = jnp.sum(activation * back, axis=1)
    dact = slot_weight * back
    d_up = (dact * gate_pre * sigmoid_gate).astype(jnp.bfloat16)
    d_gate = (dact * up_pre * sigmoid_gate * (1.0 + gate_pre * (1.0 - sigmoid_gate))).astype(
        jnp.bfloat16
    )
    act_low = activation.astype(jnp.bfloat16)
    dy_weighted = (slot_weight * dy_slots.astype(jnp.float32)).astype(jnp.bfloat16)
    contract_rows = (((0,), (0,)), ((), ()))
    grad_g = lax.dot_general(
        d_gate, x_slots, contract_rows, preferred_element_type=jnp.float32
    ).astype(jnp.bfloat16)
    grad_u = lax.dot_general(
        d_up, x_slots, contract_rows, preferred_element_type=jnp.float32
    ).astype(jnp.bfloat16)
    grad_d = lax.dot_general(
        act_low, dy_weighted, contract_rows, preferred_element_type=jnp.float32
    ).astype(jnp.bfloat16)
    dx_slots = jnp.dot(d_gate, gate_mat, preferred_element_type=jnp.float32) + jnp.dot(
        d_up, up_mat, preferred_element_type=jnp.float32
    )
    dx_tokens = jnp.einsum("bct,bcd->btd", selector, dx_slots.reshape(blocks, CAP, width)).reshape(
        -1, width
    )
    gate_tokens = jnp.einsum("bct,bc->bt", selector, slot_gate.reshape(blocks, CAP)).reshape(-1)
    return (grad_g, grad_u, grad_d, dx_tokens, gate_tokens)


def shards(hidden_in, out_grad, expert_ids, gate_values, w_gate, w_up, w_down):
    whole_x, whole_dy, whole_ids, whole_gates = (
        *sent_together((hidden_in, out_grad), "blk", 0, 1),
        lax.all_gather(expert_ids, "blk", axis=0, tiled=True),
        lax.all_gather(gate_values, "blk", axis=0, tiled=True),
    )
    blocks = whole_x.shape[0] // TOK_DEV
    first_expert = lax.axis_index("ep") * w_gate.shape[0]
    token_grad = jnp.zeros(whole_x.shape, jnp.float32)
    gate_grad = jnp.zeros(whole_ids.shape, jnp.float32)
    grads_g, grads_u, grads_d = ([], [], [])
    for local_expert in range(w_gate.shape[0]):
        selector, weight, chosen = routed(
            whole_ids, whole_gates, first_expert + local_expert, blocks
        )
        grad_g, grad_u, grad_d, dx_tokens, gate_tokens = expert_pass(
            selector,
            weight,
            whole_x,
            whole_dy,
            w_gate[local_expert],
            w_up[local_expert],
            w_down[local_expert],
            blocks,
        )
        grads_g.append(grad_g)
        grads_u.append(grad_u)
        grads_d.append(grad_d)
        token_grad = token_grad + dx_tokens
        gate_grad = gate_grad + jnp.where(chosen, gate_tokens[:, None], jnp.float32(0.0))
    part_x, part_g = side_by_side((token_grad, gate_grad), "blk", 0, 1)
    summed_x, gate_out = (
        taken_together(part_x.astype(jnp.bfloat16), "ep").astype(jnp.float32),
        taken_together(part_g.astype(jnp.bfloat16), "ep").astype(jnp.float32),
    )
    input_grad = summed_x.astype(jnp.bfloat16)
    return (input_grad, gate_out, jnp.stack(grads_g), jnp.stack(grads_u), jnp.stack(grads_d))


def solution(mesh):
    in_specs = (
        P("blk", None),
        P("blk", None),
        P("blk", None),
        P("blk", None),
        P("ep", "blk", None),
        P("ep", "blk", None),
        P("ep", "blk", None),
    )
    out_specs = (
        P("blk", None),
        P("blk", None),
        P("ep", "blk", None),
        P("ep", "blk", None),
        P("ep", "blk", None),
    )
    return jax.shard_map(shards, mesh=mesh, in_specs=in_specs, out_specs=out_specs, check_vma=False)
```

profile of v0, /device:TPU:0, one launch (start us, length us, event | category | flops | bytes accessed | tf_op | source)
XLA Modules:
  0.0 689.4 jit_solution(14464461744498951361)
XLA Ops:
  7.2 1.7 pad_maximum_fusion.4
  9.0 83.9 %all-gather = s32[64,16,2]{1,2,0:T(2,128)S(1)} all-gather(s32[1,16,2]{1,2,0:T(2,128)} %bitcast.126), channel_id=1, replica_groups=mesh['blk'=64,'ep'=2] {'blk'}, dimensions={0}, use_global_device_ids=true | all-gather | bytes 8320 | tf_op jit(solution)/shard_map/all_gather | solution.py:111
  92.9 0.2 fusion.48
  93.1 0.2 reduce_window_sum.17
  93.3 0.2 reduce_window_sum.18
  93.7 0.2 copy.58
  93.9 0.3 copy.49
  94.4 0.2 copy.61
  94.7 0.3 copy.55
  95.2 76.7 %all-gather.1 = bf16[64,16,2]{1,2,0:T(2,128)(2,1)S(1)} all-gather(bf16[1,16,2]{1,2,0:T(2,128)(2,1)} %bitcast.127), channel_id=1, replica_groups=mesh['blk'=64,'ep'=2] {'blk'}, dimensions={0}, use_global_device_ids=true | all-gather | bytes 4160 | tf_op jit(solution)/shard_map/all_gather | solution.py:112
  172.4 0.2 fusion.51
  172.6 0.1 mul.94
  172.7 0.2 copy.47
  173.1 0.2 fusion.53
  173.5 0.2 copy.53
  173.8 6.7 fusion.50
  180.5 5.6 convolution_convert_fusion.2
  186.0 5.6 convolution_convert_fusion.3
  191.6 5.6 convolution_convert_fusion
  197.2 5.6 convolution_convert_fusion.1
  202.7 10.0 %reshape.115 = bf16[768,4096]{1,0:T(8,128)(2,1)} reshape(bf16[64,12,4096]{2,1,0:T(8,128)(2,1)} %convolution_convert_fusion.2) | data formatting | bytes 12582912 | tf_op jit(solution)/shard_map/reshape | solution.py:61
  212.7 9.9 %reshape.113 = bf16[768,4096]{1,0:T(8,128)(2,1)} reshape(bf16[64,12,4096]{2,1,0:T(8,128)(2,1)} %convolution_convert_fusion.3) | data formatting | bytes 12582912 | tf_op jit(solution)/shard_map/reshape | solution.py:71
  222.6 10.1 %reshape.119 = bf16[768,4096]{1,0:T(8,128)(2,1)} reshape(bf16[64,12,4096]{2,1,0:T(8,128)(2,1)} %convolution_convert_fusion) | data formatting | bytes 12582912 | tf_op jit(solution)/shard_map/reshape | solution.py:61
  232.7 5.5 fusion.26
  238.2 0.7 copy-done.2
  238.9 2.9 fusion.17
  241.8 9.9 %reshape.118 = bf16[768,4096]{1,0:T(8,128)(2,1)} reshape(bf16[64,12,4096]{2,1,0:T(8,128)(2,1)} %convolution_convert_fusion.1) | data formatting | bytes 12582912 | tf_op jit(solution)/shard_map/reshape | solution.py:71
  251.7 5.5 fusion.28
  257.3 4.5 fusion.19
  261.8 3.2 multiply_convert_fusion.15
  265.1 1.8 fusion.21
  266.9 0.2 copy-done.3
  267.1 4.6 convolution_add_fusion.2
  271.7 10.2 %reshape.116 = bf16[64,12,4096]{2,1,0:T(8,128)(2,1)} reshape(bf16[768,4096]{1,0:T(8,128)(2,1)} %convolution_add_fusion.2) | data formatting | bytes 12582912 | tf_op jit(solution)/shard_map/reshape | solution.py:101
  281.9 6.9 %multiply_convert_fusion.13 = (bf16[768,224]{0,1:T(8,128)(2,1)S(1)}, f32[768]{0:T(1024)S(1)}, bf16[768,224]{0,1:T(8,128)(2,1)S(1)}, f32[768,224]{0,1:T(8,128)}) fusion(f32[768,224]{0,1:T(8,128)} %fusion.17, f32[768,224]{0,1:T(8,128)} %fusion.19, f32[768]{0:T(1024)S(1)} %mul.103, bf16[768,4096]{1,0:T(8,128)(2,1)} %reshape.119, bf16[2,224,4096]{2,1,0:T(8,128)(2,1)} %param.11), kind=kOutput, calls=%fused_computation.62 | convolution fusion | flops 1412381952 | bytes 10885120 | tf_op jit(solution)/shard_map/dot_general | solution.py:75
  288.8 1.8 fusion.12
  290.6 0.2 copy-done.4
  290.8 4.5 convolution_add_fusion.1
  295.4 9.8 %reshape.120 = bf16[64,12,4096]{2,1,0:T(8,128)(2,1)} reshape(bf16[768,4096]{1,0:T(8,128)(2,1)} %convolution_add_fusion.1) | data formatting | bytes 12582912 | tf_op jit(solution)/shard_map/reshape | solution.py:101
  305.2 0.2 fusion.54
  305.6 0.2 fusion.55
  305.9 0.2 copy.56
  306.2 11.5 %fusion.52 = f32[64,16,4096]{2,1,0:T(8,128)} fusion(bf16[64,12,16]{1,2,0:T(8,128)(2,1)S(1)} %copy.49, bf16[64,12,4096]{2,1,0:T(8,128)(2,1)} %reshape.116), kind=kOutput, calls=%fused_computation.92 | convolution fusion | flops 100663296 | bytes 23093248 | tf_op jit(solution)/shard_map/bct,bcd->btd/dot_general | solution.py:101
  317.7 16.2 %convolution_add_fusion = f32[64,16,4096]{2,1,0:T(8,128)} fusion(f32[64,16,4096]{2,1,0:T(8,128)} %fusion.52, bf16[64,12,16]{1,2,0:T(8,128)(2,1)S(1)} %copy.55, bf16[64,12,4096]{2,1,0:T(8,128)(2,1)} %reshape.120), kind=kOutput, calls=%fused_computation.3 | convolution fusion | flops 104857600 | bytes 39870464 | tf_op jit(solution)/shard_map/bct,bcd->btd/dot_general | solution.py:101
  333.9 11.6 %pad_maximum_fusion = f32[1024,4098]{1,0:T(8,128)} fusion(f32[1024,2]{1,0:T(8,128)S(1)} %copy.56, f32[1024,4096]{1,0:T(8,128)} %bitcast.107), kind=kLoop, calls=%fused_computation | loop fusion | flops 4196352 | bytes 33570816 | tf_op jit(solution)/shard_map/concatenate | solution.py:20
  345.6 4.5 fusion.8
  350.2 4.6 fusion.9
  354.8 2.8 fusion.6
  357.7 2.9 fusion.7
  360.7 1.9 fusion.10
  362.6 1.9 fusion.11
  364.5 2.2 pad_maximum_fusion.3
  366.7 2.2 pad_maximum_fusion.2
  368.8 290.9 %reduce-scatter.2.cloned.1.call-done = f32[16,4098]{1,0:T(8,128)} async-done(((f32[1024,4098]{1,0:T(8,128)}), f32[16,4098]{1,0:T(8,128)}) %reduce-scatter.2.cloned.1.call-update) | async-done | bytes 262288 | tf_op jit(solution)/shard_map/reduce_scatter | solution.py:21
  659.7 1.0 convert.7
  660.8 0.6 broadcast_in_dim.51
  661.4 4.2 all-to-all-start.1
  665.6 5.2 all-to-all-done.1
  670.8 0.7 broadcast_in_dim.50
  671.5 3.4 all-to-all-start
  675.0 3.7 pad_maximum_fusion.1
  678.6 0.6 convert_reduce_fusion
  679.2 2.4 all-to-all-done
  681.6 0.7 reduce_sum.61
  (83 shorter events, 2.0 us)
Async XLA Ops:
  7.2 166.6 %all-gather.4.cloned.1.call-start = ((), (), s32[]{:S(2)}) async-start(), calls=%async_computation.3 | async-start | bytes 17039360 | tf_op jit(solution)/shard_map/all_gather | solution.py:16
  8.9 650.8 %reduce-scatter.2.cloned.1.call-start = ((), (), s32[]{:S(2)}) async-start(), calls=%async_computation.4 | async-start | bytes 17571840 | tf_op jit(solution)/shard_map/reduce_scatter | solution.py:21
  232.7 5.5 copy-start.1
  232.7 6.2 copy-start.2
  238.9 22.9 %copy-start.9 = (f32[768,224]{0,1:T(8,128)}, f32[768,224]{0,1:T(8,128)S(1)}, u32[]{:S(2)}) copy-start(f32[768,224]{0,1:T(8,128)S(1)} %fusion.26) | copy-start | bytes 2064388
  251.7 5.5 copy-start
  251.7 10.1 %slice-start.4 = ((s8[6291456]{0:T(1024)(128)(4,1)}), s8[4194304]{0:T(1024)(128)(4,1)S(1)}, s32[]{:S(2)}) async-start(s8[6291456]{0:T(1024)(128)(4,1)} %bitcast.112), calls=%async_computation.9 | async-start | bytes 8388608
  257.2 4.6 slice-start.5
  257.3 4.6 copy-start.5
  265.1 2.0 copy-start.3
  281.9 6.9 %copy-start.6 = (bf16[2,224,4096]{2,1,0:T(8,128)(2,1)S(1)}, bf16[2,224,4096]{2,1,0:T(8,128)(2,1)}, u32[]{:S(2)}) copy-start(bf16[2,224,4096]{2,1,0:T(8,128)(2,1)} %param.11) | copy-start | bytes 11010052
  288.8 2.0 copy-start.4
  345.6 9.2 %slice-start.6 = ((s8[6291456]{0:T(1024)(128)(4,1)}), s8[2097152]{0:T(1024)(128)(4,1)S(1)}, s32[]{:S(2)}) async-start(s8[6291456]{0:T(1024)(128)(4,1)} %bitcast.114), calls=%async_computation.11 | async-start | bytes 4194304
  345.6 9.2 %slice-start.7 = ((s8[6291456]{0:T(1024)(128)(4,1)}), s8[4194304]{0:T(1024)(128)(4,1)S(1)}, s32[]{:S(2)}) async-start(s8[6291456]{0:T(1024)(128)(4,1)} %bitcast.114), calls=%async_computation.12 | async-start | bytes 8388608
  350.2 7.5 %slice-start.8 = ((s8[6291456]{0:T(1024)(128)(4,1)}), s8[4194304]{0:T(1024)(128)(4,1)S(1)}, s32[]{:S(2)}) async-start(s8[6291456]{0:T(1024)(128)(4,1)} %bitcast.116), calls=%async_computation.13 | async-start | bytes 8388608
  350.2 10.4 %slice-start.2 = ((s8[6291456]{0:T(1024)(128)(4,1)}), s8[4194304]{0:T(1024)(128)(4,1)S(1)}, s32[]{:S(2)}) async-start(s8[6291456]{0:T(1024)(128)(4,1)} %bitcast.110), calls=%async_computation.7 | async-start | bytes 8388608
  354.8 2.9 slice-start.9
  354.8 5.8 slice-start.3
  357.7 3.0 copy-start.10
  357.7 3.0 copy-start.11
  357.7 4.9 slice-start
  360.6 1.9 slice-start.1
  360.6 1.9 copy-start.8
  360.7 2.0 copy-start.12
  366.7 308.3 %copy-start.7 = (bf16[1,224,4096]{2,1,0:T(8,128)(2,1)S(1)}, bf16[1,224,4096]{2,1,0:T(8,128)(2,1)}, u32[]{:S(2)}) copy-start(bf16[1,224,4096]{2,1,0:T(8,128)(2,1)} %fusion.6) | copy-start | bytes 5505028
  661.4 9.4 %all-to-all-start.1 = ((bf16[2,16,2]{1,2,0:T(2,128)(2,1)}), bf16[2,16,2]{1,2,0:T(2,128)(2,1)S(1)}, u32[]{:S(2)}, u32[]{:S(2)}) async-start(bf16[2,16,2]{1,2,0:T(2,128)(2,1)} %broadcast_in_dim.51), calls=%async_computation.2 | async-start | bytes 2048 | tf_op jit(solution)/shard_map/all_to_all | solution.py:30
  671.5 10.1 %all-to-all-start = ((bf16[2,16,4096]{2,1,0:T(8,128)(2,1)}), bf16[2,16,4096]{2,1,0:T(8,128)(2,1)S(1)}, u32[]{:S(2)}, u32[]{:S(2)}) async-start(bf16[2,16,4096]{2,1,0:T(8,128)(2,1)} %broadcast_in_dim.50), calls=%async_computation.1 | async-start | bytes 524288 | tf_op jit(solution)/shard_map/all_to_all | solution.py:30
Sparse Core Ops, SparseCore 0:
  10.3 124.1 all-gather.3
  345.7 313.9 reduce-scatter.1
where the time goes:
time: 695 us; the launch traced here: 689 us
  waiting for transfers between devices  299 us (43%)
  blocking collectives  161 us (23%)
  matrix products  111 us (16%)
  local copies, waits for them, and re-layouts  72.4 us (10%)
  other arithmetic  24.3 us (3%)
  between operations  14.8 us (2%)
  starting transfers between devices  7.72 us (1%)
    reduce_scatter x1, waiting for transfers between devices, side_by_side(): lax.psum_scatter(both, axis, scatter_dimension=dim, tiled=True)  291 us
    all_gather x1, blocking collectives, shards(): lax.all_gather(expert_ids, 'blk', axis=0, tiled=True)  83.9 us
    all_gather x1, blocking collectives, shards(): lax.all_gather(gate_values, 'blk', axis=0, tiled=True)  76.7 us
    dot_general x2, matrix products, expert_pass(): jnp.einsum('bct,bcd->btd', selector, dx_slots.reshape(blocks, CAP, width))  27.8 us
    reshape x2, local copies, waits for them, and re-layouts, expert_pass(): x_slots = jnp.einsum('bct,btd->bcd', select_low, hidden_in.reshape(blocks...  20.1 us
    reshape x2, local copies, waits for them, and re-layouts, expert_pass(): dx_slots.reshape(blocks, CAP, width)  19.9 us
    reshape x2, local copies, waits for them, and re-layouts, expert_pass(): dy_slots = jnp.einsum('bct,btd->bcd', select_low, out_grad.reshape(blocks...  19.8 us
  transfers between devices with their start and end apart: 4, of which 3 were waited for; matrix products, arithmetic and copies ran while one was open for 5% of the time, Pallas kernels for 0%

commit v1 on v0

--- a/solution.py
+++ b/solution.py
@@ -5,6 +5,11 @@
 
 TOK_DEV = 16
 CAP = 12
+
+
+def swapped_in(x, axis, dim):
+    repeated = jnp.stack([x] * lax.axis_size(axis))
+    return jnp.concatenate(lax.all_to_all(repeated, axis, 0, 0), axis=dim)
 
 
 def sent_together(arrays, axis, dim, along):
@@ -108,7 +113,7 @@
 def shards(hidden_in, out_grad, expert_ids, gate_values, w_gate, w_up, w_down):
     whole_x, whole_dy, whole_ids, whole_gates = (
         *sent_together((hidden_in, out_grad), "blk", 0, 1),
-        lax.all_gather(expert_ids, "blk", axis=0, tiled=True),
+        swapped_in(expert_ids, "blk", 0),
         lax.all_gather(gate_values, "blk", axis=0, tiled=True),
     )
     blocks = whole_x.shape[0] // TOK_DEV

time: 695 us -> 658 us (0.947)
  blocking collectives: 161 us -> 82.5 us
  waiting for transfers between devices: 299 us -> 328 us
  starting transfers between devices: 7.72 us -> 17.6 us
    all_gather x1 -> x0, blocking collectives: 83.9 us -> none  [shards(): lax.all_gather(expert_ids, 'blk', axis=0, tiled=True)]
    all_gather x1, waiting for transfers between devices: 0.02 us -> 27.6 us  [sent_together(): lax.all_gather(both, axis, axis=dim, tiled=True)]
    all_to_all x0 -> x1, starting transfers between devices: none -> 9.91 us  [swapped_in(): return jnp.concatenate(lax.all_to_all(repeated, axis, 0, 0), axis=dim)]
  transfers between devices with their start and end apart: 4 -> 5, of which waited for: 3 -> 4; matrix products, arithmetic and copies ran while one was open for 5% -> 5% of each run, Pallas kernels for 0% -> 0%
where the time goes in v1:
time: 658 us; the launch traced here: 652 us
  waiting for transfers between devices  328 us (50%)
  matrix products  111 us (17%)
  blocking collectives  82.5 us (13%)
  local copies, waits for them, and re-layouts  73.8 us (11%)
  other arithmetic  24.3 us (4%)
  starting transfers between devices  17.6 us (3%)
  between operations  14.8 us (2%)
    reduce_scatter x1, waiting for transfers between devices, side_by_side(): lax.psum_scatter(both, axis, scatter_dimension=dim, tiled=True)  293 us
    all_gather x1, blocking collectives, shards(): lax.all_gather(gate_values, 'blk', axis=0, tiled=True)  82.5 us
    dot_general x2, matrix products, expert_pass(): jnp.einsum('bct,bcd->btd', selector, dx_slots.reshape(blocks, CAP, width))  27.8 us
    all_gather x1, waiting for transfers between devices, sent_together(): lax.all_gather(both, axis, axis=dim, tiled=True)  27.6 us
    reshape x2, local copies, waits for them, and re-layouts, expert_pass(): x_slots = jnp.einsum('bct,btd->bcd', select_low, hidden_in.reshape(blocks...  20.1 us
    reshape x2, local copies, waits for them, and re-layouts, expert_pass(): dx_slots.reshape(blocks, CAP, width)  19.9 us
    reshape x2, local copies, waits for them, and re-layouts, expert_pass(): dy_slots = jnp.einsum('bct,btd->bcd', select_low, out_grad.reshape(blocks...  19.8 us
  transfers between devices with their start and end apart: 5, of which 4 were waited for; matrix products, arithmetic and copies ran while one was open for 5% of the time, Pallas kernels for 0%

profile of v1, /device:TPU:0, one launch (start us, length us, event | category | flops | bytes accessed | tf_op | source)
XLA Modules:
  0.0 652.3 jit_solution(10306818015284191074)
XLA Ops:
  7.2 1.7 pad_maximum_fusion.4
  8.9 1.3 stack.20
  10.3 9.9 %all-to-all-start = ((s32[64,16,2]{1,2,0:T(2,128)}), s32[64,16,2]{1,2,0:T(2,128)S(1)}, u32[]{:S(2)}, u32[]{:S(2)}) async-start(s32[64,16,2]{1,2,0:T(2,128)} %stack.20), calls=%async_computation | async-start | bytes 131072 | tf_op jit(solution)/shard_map/all_to_all | solution.py:12
  20.2 82.5 %all-gather = bf16[64,16,2]{1,2,0:T(2,128)(2,1)S(1)} all-gather(bf16[1,16,2]{1,2,0:T(2,128)(2,1)} %bitcast.125), channel_id=1, replica_groups=mesh['blk'=64,'ep'=2] {'blk'}, dimensions={0}, use_global_device_ids=true | all-gather | bytes 4160 | tf_op jit(solution)/shard_map/all_gather | solution.py:117
  103.0 0.2 fusion.48
  103.3 0.2 reduce_window_sum.17
  103.6 0.2 copy.63
  103.9 0.3 copy.54
  104.6 0.2 copy.66
  104.8 0.3 copy.60
  105.5 0.2 fusion.51
  105.9 0.2 copy.52
  106.2 0.2 fusion.53
  106.6 0.2 copy.58
  106.9 27.6 %all-gather.3.cloned.1.call-done = bf16[1024,8192]{1,0:T(8,128)(2,1)} async-done(((bf16[16,8192]{1,0:T(8,128)(2,1)}), bf16[1024,8192]{1,0:T(8,128)(2,1)}) %all-gather.3.cloned.1.call-update) | async-done | bytes 16777232 | tf_op jit(solution)/shard_map/all_gather | solution.py:21
  134.5 6.7 %fusion.50 = (bf16[1024,4096]{1,0:T(8,128)(2,1)S(1)}, bf16[1024,4096]{1,0:T(8,128)(2,1)S(1)}) fusion(bf16[1024,8192]{1,0:T(8,128)(2,1)} %all-gather.3.cloned.1.call-done), kind=kLoop, calls=%fused_computation.90 | loop fusion | bytes 33554432 | tf_op jit(solution)/shard_map/split | solution.py:21
  141.2 5.6 convolution_convert_fusion.2
  146.8 5.6 convolution_convert_fusion.3
  152.3 5.6 convolution_convert_fusion
  157.9 5.6 convolution_convert_fusion.1
  163.4 10.0 %reshape.116 = bf16[768,4096]{1,0:T(8,128)(2,1)} reshape(bf16[64,12,4096]{2,1,0:T(8,128)(2,1)} %convolution_convert_fusion.2) | data formatting | bytes 12582912 | tf_op jit(solution)/shard_map/reshape | solution.py:66
  173.4 9.9 %reshape.114 = bf16[768,4096]{1,0:T(8,128)(2,1)} reshape(bf16[64,12,4096]{2,1,0:T(8,128)(2,1)} %convolution_convert_fusion.3) | data formatting | bytes 12582912 | tf_op jit(solution)/shard_map/reshape | solution.py:76
  183.3 10.1 %reshape.120 = bf16[768,4096]{1,0:T(8,128)(2,1)} reshape(bf16[64,12,4096]{2,1,0:T(8,128)(2,1)} %convolution_convert_fusion) | data formatting | bytes 12582912 | tf_op jit(solution)/shard_map/reshape | solution.py:66
  193.4 5.5 fusion.26
  198.9 0.7 copy-done.2
  199.6 2.9 fusion.17
  202.5 9.9 %reshape.119 = bf16[768,4096]{1,0:T(8,128)(2,1)} reshape(bf16[64,12,4096]{2,1,0:T(8,128)(2,1)} %convolution_convert_fusion.1) | data formatting | bytes 12582912 | tf_op jit(solution)/shard_map/reshape | solution.py:76
  212.4 5.5 fusion.28
  218.0 4.5 fusion.19
  222.6 3.2 multiply_convert_fusion.15
  225.8 1.8 fusion.21
  227.6 0.2 copy-done.3
  227.8 4.6 convolution_add_fusion.2
  232.4 10.2 %reshape.117 = bf16[64,12,4096]{2,1,0:T(8,128)(2,1)} reshape(bf16[768,4096]{1,0:T(8,128)(2,1)} %convolution_add_fusion.2) | data formatting | bytes 12582912 | tf_op jit(solution)/shard_map/reshape | solution.py:106
  242.6 6.9 %multiply_convert_fusion.13 = (bf16[768,224]{0,1:T(8,128)(2,1)S(1)}, f32[768]{0:T(1024)S(1)}, bf16[768,224]{0,1:T(8,128)(2,1)S(1)}, f32[768,224]{0,1:T(8,128)}) fusion(f32[768,224]{0,1:T(8,128)} %fusion.17, f32[768,224]{0,1:T(8,128)} %fusion.19, f32[768]{0:T(1024)S(1)} %mul.103, bf16[768,4096]{1,0:T(8,128)(2,1)} %reshape.120, bf16[2,224,4096]{2,1,0:T(8,128)(2,1)} %param.11), kind=kOutput, calls=%fused_computation.62 | convolution fusion | flops 1412381952 | bytes 10885120 | tf_op jit(solution)/shard_map/dot_general | solution.py:80
  249.5 1.8 fusion.12
  251.4 0.2 copy-done.4
  251.6 4.5 convolution_add_fusion.1
  256.1 9.8 %reshape.121 = bf16[64,12,4096]{2,1,0:T(8,128)(2,1)} reshape(bf16[768,4096]{1,0:T(8,128)(2,1)} %convolution_add_fusion.1) | data formatting | bytes 12582912 | tf_op jit(solution)/shard_map/reshape | solution.py:106
  265.9 0.2 fusion.54
  266.3 0.2 fusion.55
  266.7 0.2 copy.61
  266.9 11.5 %fusion.52 = f32[64,16,4096]{2,1,0:T(8,128)} fusion(bf16[64,12,16]{1,2,0:T(8,128)(2,1)S(1)} %copy.54, bf16[64,12,4096]{2,1,0:T(8,128)(2,1)} %reshape.117), kind=kOutput, calls=%fused_computation.92 | convolution fusion | flops 100663296 | bytes 23093248 | tf_op jit(solution)/shard_map/bct,bcd->btd/dot_general | solution.py:106
  278.4 16.2 %convolution_add_fusion = f32[64,16,4096]{2,1,0:T(8,128)} fusion(f32[64,16,4096]{2,1,0:T(8,128)} %fusion.52, bf16[64,12,16]{1,2,0:T(8,128)(2,1)S(1)} %copy.60, bf16[64,12,4096]{2,1,0:T(8,128)(2,1)} %reshape.121), kind=kOutput, calls=%fused_computation.3 | convolution fusion | flops 104857600 | bytes 39870464 | tf_op jit(solution)/shard_map/bct,bcd->btd/dot_general | solution.py:106
  294.7 11.6 %pad_maximum_fusion = f32[1024,4098]{1,0:T(8,128)} fusion(f32[1024,2]{1,0:T(8,128)S(1)} %copy.61, f32[1024,4096]{1,0:T(8,128)} %bitcast.106), kind=kLoop, calls=%fused_computation | loop fusion | flops 4196352 | bytes 33570816 | tf_op jit(solution)/shard_map/concatenate | solution.py:25
  306.3 4.5 fusion.8
  310.9 4.5 fusion.9
  315.5 2.8 fusion.6
  318.3 2.9 fusion.7
  321.3 1.9 fusion.10
  323.3 1.9 fusion.11
  325.2 2.2 pad_maximum_fusion.3
  327.3 2.2 pad_maximum_fusion.2
  329.5 293.2 %reduce-scatter.2.cloned.1.call-done = f32[16,4098]{1,0:T(8,128)} async-done(((f32[1024,4098]{1,0:T(8,128)}), f32[16,4098]{1,0:T(8,128)}) %reduce-scatter.2.cloned.1.call-update) | async-done | bytes 262288 | tf_op jit(solution)/shard_map/reduce_scatter | solution.py:26
  622.7 1.0 convert.5
  623.8 0.6 broadcast_in_dim.51
  624.3 4.2 all-to-all-start.2
  628.5 5.2 all-to-all-done.2
  633.7 0.7 broadcast_in_dim.50
  634.4 3.4 all-to-all-start.1
  637.9 3.7 pad_maximum_fusion.1
  641.6 0.6 convert_reduce_fusion
  642.1 2.4 all-to-all-done.1
  644.5 0.7 reduce_sum.61
  (85 shorter events, 2.3 us)
Async XLA Ops:
  7.2 127.3 %all-gather.3.cloned.1.call-start = ((), (), s32[]{:S(2)}) async-start(), calls=%async_computation.4 | async-start | bytes 17039360 | tf_op jit(solution)/shard_map/all_gather | solution.py:21
  10.3 92.7 %all-to-all-start = ((s32[64,16,2]{1,2,0:T(2,128)}), s32[64,16,2]{1,2,0:T(2,128)S(1)}, u32[]{:S(2)}, u32[]{:S(2)}) async-start(s32[64,16,2]{1,2,0:T(2,128)} %stack.20), calls=%async_computation | async-start | bytes 131072 | tf_op jit(solution)/shard_map/all_to_all | solution.py:12
  20.2 602.5 %reduce-scatter.2.cloned.1.call-start = ((), (), s32[]{:S(2)}) async-start(), calls=%async_computation.5 | async-start | bytes 17571840 | tf_op jit(solution)/shard_map/reduce_scatter | solution.py:26
  193.4 5.5 copy-start.1
  193.4 6.2 copy-start.2
  199.6 22.9 %copy-start.9 = (f32[768,224]{0,1:T(8,128)}, f32[768,224]{0,1:T(8,128)S(1)}, u32[]{:S(2)}) copy-start(f32[768,224]{0,1:T(8,128)S(1)} %fusion.26) | copy-start | bytes 2064388
  212.4 5.5 copy-start
  212.4 10.1 %slice-start.4 = ((s8[6291456]{0:T(1024)(128)(4,1)}), s8[4194304]{0:T(1024)(128)(4,1)S(1)}, s32[]{:S(2)}) async-start(s8[6291456]{0:T(1024)(128)(4,1)} %bitcast.111), calls=%async_computation.10 | async-start | bytes 8388608
  218.0 4.6 slice-start.5
  218.0 4.6 copy-start.5
  225.8 2.0 copy-start.3
  242.6 6.9 %copy-start.6 = (bf16[2,224,4096]{2,1,0:T(8,128)(2,1)S(1)}, bf16[2,224,4096]{2,1,0:T(8,128)(2,1)}, u32[]{:S(2)}) copy-start(bf16[2,224,4096]{2,1,0:T(8,128)(2,1)} %param.11) | copy-start | bytes 11010052
  249.5 2.0 copy-start.4
  306.3 9.1 %slice-start.6 = ((s8[6291456]{0:T(1024)(128)(4,1)}), s8[2097152]{0:T(1024)(128)(4,1)S(1)}, s32[]{:S(2)}) async-start(s8[6291456]{0:T(1024)(128)(4,1)} %bitcast.113), calls=%async_computation.12 | async-start | bytes 4194304
  306.3 9.1 %slice-start.7 = ((s8[6291456]{0:T(1024)(128)(4,1)}), s8[4194304]{0:T(1024)(128)(4,1)S(1)}, s32[]{:S(2)}) async-start(s8[6291456]{0:T(1024)(128)(4,1)} %bitcast.113), calls=%async_computation.13 | async-start | bytes 8388608
  310.9 7.4 %slice-start.8 = ((s8[6291456]{0:T(1024)(128)(4,1)}), s8[4194304]{0:T(1024)(128)(4,1)S(1)}, s32[]{:S(2)}) async-start(s8[6291456]{0:T(1024)(128)(4,1)} %bitcast.115), calls=%async_computation.14 | async-start | bytes 8388608
  310.9 10.4 %slice-start.2 = ((s8[6291456]{0:T(1024)(128)(4,1)}), s8[4194304]{0:T(1024)(128)(4,1)S(1)}, s32[]{:S(2)}) async-start(s8[6291456]{0:T(1024)(128)(4,1)} %bitcast.109), calls=%async_computation.8 | async-start | bytes 8388608
  315.5 2.9 slice-start.9
  315.5 5.8 slice-start.3
  318.3 3.0 copy-start.10
  318.3 3.0 copy-start.11
  318.3 4.9 slice-start
  321.3 1.9 slice-start.1
  321.3 1.9 copy-start.8
  321.3 2.0 copy-start.12
  327.3 310.5 %copy-start.7 = (bf16[1,224,4096]{2,1,0:T(8,128)(2,1)S(1)}, bf16[1,224,4096]{2,1,0:T(8,128)(2,1)}, u32[]{:S(2)}) copy-start(bf16[1,224,4096]{2,1,0:T(8,128)(2,1)} %fusion.6) | copy-start | bytes 5505028
  624.3 9.4 %all-to-all-start.2 = ((bf16[2,16,2]{1,2,0:T(2,128)(2,1)}), bf16[2,16,2]{1,2,0:T(2,128)(2,1)S(1)}, u32[]{:S(2)}, u32[]{:S(2)}) async-start(bf16[2,16,2]{1,2,0:T(2,128)(2,1)} %broadcast_in_dim.51), calls=%async_computation.3 | async-start | bytes 2048 | tf_op jit(solution)/shard_map/all_to_all | solution.py:35
  634.4 10.1 %all-to-all-start.1 = ((bf16[2,16,4096]{2,1,0:T(8,128)(2,1)}), bf16[2,16,4096]{2,1,0:T(8,128)(2,1)S(1)}, u32[]{:S(2)}, u32[]{:S(2)}) async-start(bf16[2,16,4096]{2,1,0:T(8,128)(2,1)} %broadcast_in_dim.50), calls=%async_computation.2 | async-start | bytes 524288 | tf_op jit(solution)/shard_map/all_to_all | solution.py:35
Sparse Core Ops, SparseCore 0:
  10.3 124.1 all-gather.2
  306.4 316.2 reduce-scatter.1
